TPU v7x, 256 devices: a whole 4x4x8 slice. The times are simulated.
256 devices in a mesh: bank: 16 (over z, core), zero: 16 (over y, x).
Axes of the slice: x: 4, y: 4, z: 8, core: 2. Of those that a mesh axis runs over, the one named last changes fastest.
Arguments:
- master_down: float32 [64, 1024, 2048], P('bank', None, 'zero'), may hold values from -0.25 to 0.25
- second_down: bfloat16 [64, 1024, 2048], P('bank', None, 'zero'), may hold values from -0.09375 to 0.09375
- router_weight: float32 [2048, 64], P('zero', 'bank'), may hold values from -0.125 to 0.125
- router_gain: float32 [2048], P('zero'), may hold values from 0.25 to 1.75
Outputs:
- final_down: bfloat16 [64, 1024, 2048], P('bank')
- scale_down: float32 [64, 1024], P('bank')
- serve_router: bfloat16 [2048, 64], replicated
All inputs are finite; a program needn't handle non-finite values. Where the computation divides by a largest or mean magnitude, that divisor is 1e-20 or more.
Results may differ from a plain program's by a relative error of at most 0.001.
Values may be sent and summed in bfloat16 or wider, within the bound.
A program may use at most 128 MiB of HBM per device.

v0:
```python
import jax
import jax.numpy as jnp
from jax import lax
from jax.sharding import PartitionSpec as P


def from_everyone(value, axis):
    count = lax.axis_size(axis)
    return lax.all_to_all(
        jnp.broadcast_to(value[None], (count, *value.shape)), axis, 0, 0, tiled=True
    )


def over_copies(value, axis):
    everything = from_everyone(value, axis)
    return jnp.max(everything, axis=0)


def joined_along(pieces, dim):
    pieces = jnp.moveaxis(pieces, 0, dim)
    dims = pieces.shape
    return pieces.reshape(*dims[:dim], dims[dim] * dims[dim + 1], *dims[dim + 2 :])


def collect(value, axis, dim):
    return joined_along(from_everyone(value, axis), dim)


def shards(master_down, second_down, router_weight, router_gain):
    merged_down = master_down + second_down.astype(jnp.float32)
    scale_down = over_copies(jnp.max(jnp.abs(merged_down), axis=2), "zero")
    narrow_down = (merged_down / jnp.expand_dims(scale_down, 2)).astype(jnp.bfloat16)
    final_down = lax.all_gather(narrow_down, "zero", axis=2, tiled=True)
    part_router = (router_weight * router_gain[:, None]).astype(jnp.bfloat16)
    row_router = collect(part_router, "zero", 0)
    serve_router = lax.all_gather(row_router, "bank", axis=1, tiled=True)
    return (final_down, scale_down, serve_router)


def solution(mesh):
    return jax.shard_map(
        shards,
        mesh=mesh,
        in_specs=(P("bank", None, "zero"), P("bank", None, "zero"), P("zero", "bank"), P("zero")),
        out_specs=(P("bank", None, None), P("bank", None), P()),
        check_vma=False,
    )
```

profile of v0, /device:TPU:2, one launch (start us, length us, event | category | flops | bytes accessed | tf_op | source)
XLA Modules:
  0.0 171.8 jit_solution(3253551120182133146)
XLA Ops:
  7.2 0.0 copy-start
  7.2 0.0 copy-start.1
  7.2 0.0 all-gather.3.cloned.1.call-start
  7.2 2.6 %abs_reduce_fusion = f32[4,1024]{1,0:T(4,128)S(1)} fusion(f32[4,1024,128]{2,1,0:T(8,128)} %param.4, bf16[4,1024,128]{2,1,0:T(8,128)(2,1)} %param.5), kind=kLoop, calls=%fused_computation.1 | loop fusion | flops 2093056 | bytes 3162112 | tf_op jit(solution)/shard_map/reduce_max | solution.py:31
  9.9 14.6 %all_to_all.10 = f32[16,4,1024]{2,1,0:T(4,128)S(1)} all-to-all(f32[16,4,1024]{2,1,0:T(4,128)S(1)} %broadcast_in_dim.4), channel_id=1, replica_groups=mesh['bank'=16,'zero'=16] {'zero'}, dimensions={0} | all-to-all | bytes 524288 | tf_op jit(solution)/shard_map/all_to_all | solution.py:9
  24.5 0.1 reduce_max.19
  24.6 0.0 copy-done
  24.6 0.0 copy-done.1
  24.6 0.0 copy-start.2
  24.6 0.0 copy-start.3
  24.6 0.0 copy-start.4
  24.6 1.5 divide_convert_fusion
  26.1 0.0 copy-done.2
  26.1 0.0 all-gather.3.cloned.1.call-update
  26.2 0.0 copy-done.3
  26.2 0.0 copy-done.4
  26.2 10.5 %all_to_all.11 = bf16[16,128,4]{1,2,0:T(4,128)(2,1)S(1)} all-to-all(bf16[16,128,4]{1,2,0:T(4,128)(2,1)S(1)} %broadcast_in_dim.5), channel_id=1, replica_groups=mesh['bank'=16,'zero'=16] {'zero'}, dimensions={0} | all-to-all | bytes 32768 | tf_op jit(solution)/shard_map/all_to_all | solution.py:9
  36.7 20.7 %all-gather = bf16[16,4,2048]{2,1,0:T(4,128)(2,1)S(1)} all-gather(bf16[1,4,2048]{2,1,0:T(4,128)(2,1)S(1)} %bitcast.7), channel_id=1, replica_groups=mesh['bank'=16,'zero'=16] {'bank'}, dimensions={0}, use_global_device_ids=true | all-gather | bytes 278528 | tf_op jit(solution)/shard_map/all_gather | solution.py:36
  57.4 0.8 reshape.15
  58.1 92.7 %all-gather.3.cloned.1.call-done = bf16[4,1024,2048]{2,1,0:T(8,128)(2,1)} async-done(((bf16[4,1024,128]{2,1,0:T(8,128)(2,1)}), bf16[4,1024,2048]{2,1,0:T(8,128)(2,1)}) %all-gather.3.cloned.1.call-update) | async-done | bytes 16777232 | tf_op jit(solution)/shard_map/all_gather | solution.py:33
  150.8 14.2 %copy.10 = bf16[4,1024,2048]{2,1,0:T(8,128)(2,1)} copy(bf16[4,1024,2048]{2,1,0:T(8,128)(2,1)} %all-gather.3.cloned.1.call-done) | data formatting | bytes 33554432
  (3 shorter events, 0.1 us)
Async XLA Ops:
  7.2 17.4 %copy-start = (f32[4,1024,128]{2,1,0:T(8,128)S(1)}, f32[4,1024,128]{2,1,0:T(8,128)}, u32[]{:S(2)}) copy-start(f32[4,1024,128]{2,1,0:T(8,128)} %param.4) | copy-start | bytes 6291460
  7.2 17.4 %copy-start.1 = (bf16[4,1024,128]{2,1,0:T(8,128)(2,1)S(1)}, bf16[4,1024,128]{2,1,0:T(8,128)(2,1)}, u32[]{:S(2)}) copy-start(bf16[4,1024,128]{2,1,0:T(8,128)(2,1)} %param.5) | copy-start | bytes 3145732
  7.2 143.6 %all-gather.3.cloned.1.call-start = ((), (), s32[]{:S(2)}) async-start(), calls=%async_computation.2 | async-start | bytes 17825792 | tf_op jit(solution)/shard_map/all_gather | solution.py:33
  24.6 1.6 copy-start.2
  24.6 1.6 copy-start.3
  24.6 1.6 copy-start.4
Sparse Core Ops, SparseCore 0:
  26.3 124.4 all-gather.2
where the time goes:
time: 172 us
  waiting for transfers between devices  92.7 us (54%)
  blocking collectives  45.8 us (27%)
  local copies, waits for them, and re-layouts  15 us (9%)
  between operations  14.1 us (8%)
  other arithmetic  4.21 us (2%)
    all_gather x1, waiting for transfers between devices, shards(): final_down = lax.all_gather(narrow_down, 'zero', axis=2, tiled=True)  92.7 us
    all_to_all x2, blocking collectives, from_everyone(): lax.all_to_all(jnp.broadcast_to(value[None], (count, *value.shape)), axis...  25.1 us
    all_gather x1, blocking collectives, shards(): serve_router = lax.all_gather(row_router, 'bank', axis=1, tiled=True)  20.7 us
    unnamed x12, local copies, waits for them, and re-layouts  14.9 us
  transfers between devices with their start and end apart: 1, of which 1 were waited for; matrix products, arithmetic and copies ran while one was open for 0% of the time, Pallas kernels for 0%

commit v1 on v0

--- a/solution.py
+++ b/solution.py
@@ -30,7 +30,7 @@
     merged_down = master_down + second_down.astype(jnp.float32)
     scale_down = over_copies(jnp.max(jnp.abs(merged_down), axis=2), "zero")
     narrow_down = (merged_down / jnp.expand_dims(scale_down, 2)).astype(jnp.bfloat16)
-    final_down = lax.all_gather(narrow_down, "zero", axis=2, tiled=True)
+    final_down = jnp.concatenate(lax.all_gather(narrow_down, "zero"), axis=2)
     part_router = (router_weight * router_gain[:, None]).astype(jnp.bfloat16)
     row_router = collect(part_router, "zero", 0)
     serve_router = lax.all_gather(row_router, "bank", axis=1, tiled=True)

time: 172 us -> 166 us (0.965)
  waiting for transfers between devices: 92.7 us -> 84.4 us
    reshape x0 -> x1, local copies, waits for them, and re-layouts: none -> 15.3 us  [shards(): final_down = jnp.concatenate(lax.all_gather(narrow_down, 'zero'), axis=2)]
    unnamed x12 -> x11, local copies, waits for them, and re-layouts: 14.9 us -> 0.79 us
    all_gather x1, waiting for transfers between devices: 92.7 us -> 84.3 us  [shards(): final_down = jnp.concatenate(lax.all_gather(narrow_down, 'zero'), axis=2)]
where the time goes in v1:
time: 166 us; the launch traced here: 165 us
  waiting for transfers between devices  84.4 us (51%)
  blocking collectives  45.8 us (28%)
  local copies, waits for them, and re-layouts  16.2 us (10%)
  between operations  14.1 us (8%)
  other arithmetic  4.21 us (3%)
    all_gather x1, waiting for transfers between devices, shards(): final_down = jnp.concatenate(lax.all_gather(narrow_down, 'zero'), axis=2)  84.3 us
    all_to_all x2, blocking collectives, from_everyone(): lax.all_to_all(jnp.broadcast_to(value[None], (count, *value.shape)), axis...  25.1 us
    all_gather x1, blocking collectives, shards(): serve_router = lax.all_gather(row_router, 'bank', axis=1, tiled=True)  20.7 us
    reshape x1, local copies, waits for them, and re-layouts, shards(): final_down = jnp.concatenate(lax.all_gather(narrow_down, 'zero'), axis=2)  15.3 us
  transfers between devices with their start and end apart: 1, of which 1 were waited for; matrix products, arithmetic and copies ran while one was open for 0% of the time, Pallas kernels for 0%

profile of v1, /device:TPU:2, one launch (start us, length us, event | category | flops | bytes accessed | tf_op | source)
XLA Modules:
  0.0 164.7 jit_solution(3314378420289406427)
XLA Ops:
  7.2 0.0 copy-start
  7.2 0.0 copy-start.1
  7.2 0.0 all-gather.4.cloned.1.call-start
  7.2 2.6 %abs_reduce_fusion = f32[4,1024]{1,0:T(4,128)S(1)} fusion(f32[4,1024,128]{2,1,0:T(8,128)} %param.4, bf16[4,1024,128]{2,1,0:T(8,128)(2,1)} %param.5), kind=kLoop, calls=%fused_computation.2 | loop fusion | flops 2093056 | bytes 3162112 | tf_op jit(solution)/shard_map/reduce_max | solution.py:31
  9.9 14.6 %all_to_all.10 = f32[16,4,1024]{2,1,0:T(4,128)S(1)} all-to-all(f32[16,4,1024]{2,1,0:T(4,128)S(1)} %broadcast_in_dim.4), channel_id=1, replica_groups=mesh['bank'=16,'zero'=16] {'zero'}, dimensions={0} | all-to-all | bytes 524288 | tf_op jit(solution)/shard_map/all_to_all | solution.py:9
  24.5 0.1 reduce_max.19
  24.6 0.0 copy-done
  24.6 0.0 copy-done.1
  24.6 0.0 copy-start.2
  24.6 0.0 copy-start.3
  24.6 0.0 copy-start.4
  24.6 1.5 divide_convert_fusion
  26.1 0.0 copy-done.2
  26.1 0.0 all-gather.4.cloned.1.call-update
  26.2 0.0 copy-done.3
  26.2 0.0 copy-done.4
  26.2 10.5 %all_to_all.11 = bf16[16,128,4]{1,2,0:T(4,128)(2,1)S(1)} all-to-all(bf16[16,128,4]{1,2,0:T(4,128)(2,1)S(1)} %broadcast_in_dim.5), channel_id=1, replica_groups=mesh['bank'=16,'zero'=16] {'zero'}, dimensions={0} | all-to-all | bytes 32768 | tf_op jit(solution)/shard_map/all_to_all | solution.py:9
  36.7 20.7 %all-gather.1 = bf16[16,4,2048]{2,1,0:T(4,128)(2,1)S(1)} all-gather(bf16[1,4,2048]{2,1,0:T(4,128)(2,1)S(1)} %bitcast.16), channel_id=1, replica_groups=mesh['bank'=16,'zero'=16] {'bank'}, dimensions={0}, use_global_device_ids=true | all-gather | bytes 278528 | tf_op jit(solution)/shard_map/all_gather | solution.py:36
  57.4 0.8 reshape.24
  58.1 84.3 %all-gather.4.cloned.1.call-done = bf16[64,1024,128]{2,1,0:T(8,128)(2,1)} async-done(((bf16[4,1024,128]{2,1,0:T(8,128)(2,1)}), bf16[64,1024,128]{2,1,0:T(8,128)(2,1)}) %all-gather.4.cloned.1.call-update) | async-done | bytes 16777232 | tf_op jit(solution)/shard_map/all_gather | solution.py:33
  142.5 15.3 %copy.15 = bf16[16,4,128,8,128]{4,3,0,2,1:T(8,128)(2,1)} copy(bf16[16,4,128,8,128]{4,3,2,1,0:T(8,128)(2,1)} %bitcast.13) | data formatting | bytes 33554432 | tf_op jit(solution)/shard_map/reshape | solution.py:33
  (3 shorter events, 0.1 us)
Async XLA Ops:
  7.2 17.4 %copy-start = (f32[4,1024,128]{2,1,0:T(8,128)S(1)}, f32[4,1024,128]{2,1,0:T(8,128)}, u32[]{:S(2)}) copy-start(f32[4,1024,128]{2,1,0:T(8,128)} %param.4) | copy-start | bytes 6291460
  7.2 17.4 %copy-start.1 = (bf16[4,1024,128]{2,1,0:T(8,128)(2,1)S(1)}, bf16[4,1024,128]{2,1,0:T(8,128)(2,1)}, u32[]{:S(2)}) copy-start(bf16[4,1024,128]{2,1,0:T(8,128)(2,1)} %param.5) | copy-start | bytes 3145732
  7.2 135.3 %all-gather.4.cloned.1.call-start = ((), (), s32[]{:S(2)}) async-start(), calls=%async_computation.2 | async-start | bytes 17825792 | tf_op jit(solution)/shard_map/all_gather | solution.py:33
  24.6 1.6 copy-start.2
  24.6 1.6 copy-start.3
  24.6 1.6 copy-start.4
Sparse Core Ops, SparseCore 0:
  26.3 116.1 all-gather.3
